TPU v7x, 32 devices: a whole 2x2x4 slice. The times are simulated.
32 devices in a mesh: dp: 8 (over y, x, core), tp: 4 (over z).
Axes of the slice: x: 2, y: 2, z: 4, core: 2. Of those that a mesh axis runs over, the one named last changes fastest.
Arguments:
- embeddings: bfloat16 [768, 192, 256], P(('dp', 'tp')), may hold values from -6 to 6
- projection: bfloat16 [256, 16], replicated, may hold values from -0.375 to 0.375
- compress: bfloat16 [256, 4], replicated, may hold values from -0.375 to 0.375
- w_up: bfloat16 [4096, 4096], P(None, 'tp'), may hold values from -0.09375 to 0.09375
- w_down: bfloat16 [4096, 768], P('tp'), may hold values from -0.125 to 0.125
- output_norm_gain: float32 [1536], P('tp'), may hold values from 0.25 to 1.75
- out_grad: bfloat16 [768, 1536], P('dp', 'tp'), may hold values from -6 to 6
Outputs:
- block_result: bfloat16 [768, 1536], P('dp', 'tp')
- grad_down: float32 [4096, 768], P(('tp', 'dp'))
All inputs are finite; a program needn't handle non-finite values.
Results may differ from a plain program's by a relative error of at most 0.017.
Values may be sent and summed in bfloat16 or wider, within the bound.
A program may use at most 64 MiB of HBM per device.

v0:
```python
import jax
import jax.numpy as jnp
from jax import lax
from jax.sharding import PartitionSpec as P


def merged(value, axis, join):
    pieces = jax.tree.map(lambda part: lax.all_gather(part, axis), value)
    head = jax.tree.map(lambda part: part[0], pieces)
    tail = jax.tree.map(lambda part: part[1:], pieces)
    subtotal, _ = lax.scan(lambda subtotal, share: (join(subtotal, share), None), head, tail)
    return subtotal


def chan_merge(left, right):
    count_a, mean_a, dev_a = left
    count_b, mean_b, dev_b = right
    total = count_a + count_b
    delta = mean_b - mean_a
    row_average = mean_a + delta * (count_b / total)
    dev = dev_a + dev_b + delta * delta * (count_a * count_b / total)
    return (total, row_average, dev)


def alternate(mlp_part, lcb_part, groups):
    rows = mlp_part.shape[0]
    return jnp.concatenate(
        [mlp_part.reshape(rows, groups, -1), lcb_part.reshape(rows, groups, -1)], axis=2
    ).reshape(rows, -1)


def on_device(embeddings, projection, compress, w_up, w_down, output_norm_gain, out_grad):
    samples = embeddings.shape[0]
    pairs = jnp.einsum(
        "sef,fk->sek", embeddings, projection, preferred_element_type=jnp.float32
    ).astype(jnp.bfloat16)
    inter = jnp.einsum(
        "sek,sef->skf", pairs, embeddings, preferred_element_type=jnp.float32
    ).reshape(samples, -1)
    center = inter - jnp.mean(inter, axis=1, keepdims=True)
    spread = jnp.mean(center * center, axis=1, keepdims=True)
    normed = (center / jnp.sqrt(spread + 1e-05)).astype(jnp.bfloat16)
    lcb = jnp.einsum(
        "sef,fj->sje", embeddings, compress, preferred_element_type=jnp.float32
    ).reshape(samples, -1)
    hidden = jax.nn.gelu(
        jnp.dot(
            lax.all_gather(normed, "tp", axis=0, tiled=True),
            w_up,
            preferred_element_type=jnp.float32,
        ),
        approximate=True,
    ).astype(jnp.bfloat16)
    group_rows = hidden.shape[0]
    tp_count = lax.axis_size("tp")
    position = lax.axis_index("tp")
    mlp = jnp.dot(hidden, w_down, preferred_element_type=jnp.float32)
    mlp_width = mlp.shape[1]
    full_width = mlp_width + lcb.shape[1]
    width = full_width // tp_count
    placed = lax.dynamic_update_slice(
        jnp.zeros((group_rows, lcb.shape[1]), jnp.float32), lcb, (position * samples, jnp.int32(0))
    )
    term = alternate(mlp, placed, tp_count)
    mixed_rows = lax.psum_scatter(
        term.astype(jnp.bfloat16), "tp", scatter_dimension=1, tiled=True
    ).astype(jnp.float32)
    own_mean = jnp.mean(mixed_rows, axis=1)
    own_dev = jnp.sum((mixed_rows - own_mean[:, None]) ** 2, axis=1)
    own_count = jnp.full((), width, jnp.float32)
    total, row_average, dev = merged((own_count, own_mean, own_dev), "tp", chan_merge)
    inverse_deviation = 1.0 / jnp.sqrt(dev[:, None] / total + 1e-05)
    centered_rows = (mixed_rows - row_average[:, None]) * inverse_deviation
    block_result = (centered_rows * output_norm_gain).astype(jnp.bfloat16)
    scaled_rows = out_grad.astype(jnp.float32) * output_norm_gain
    sum_one, sum_two = lax.psum(
        (jnp.sum(scaled_rows, axis=1), jnp.sum(scaled_rows * centered_rows, axis=1)), "tp"
    )
    first_moment = (sum_one / full_width)[:, None]
    second_moment = (sum_two / full_width)[:, None]
    local_grad = (
        (scaled_rows - first_moment - centered_rows * second_moment) * inverse_deviation
    ).astype(jnp.bfloat16)
    mixed_gradient = lax.all_gather(local_grad, "tp", axis=1, tiled=True)
    group_mlp = mlp_width // tp_count
    mlp_grad = mixed_gradient.reshape(group_rows, tp_count, -1)[:, :, :group_mlp].reshape(
        group_rows, -1
    )
    grad_down = lax.psum_scatter(
        jnp.einsum("rh,rc->hc", hidden, mlp_grad, preferred_element_type=jnp.float32).astype(
            jnp.bfloat16
        ),
        "dp",
        scatter_dimension=0,
        tiled=True,
    ).astype(jnp.float32)
    return (block_result, grad_down)


def solution(mesh):
    return jax.shard_map(
        on_device,
        mesh=mesh,
        in_specs=(
            P(("dp", "tp"), None, None),
            P(),
            P(),
            P(None, "tp"),
            P("tp", None),
            P("tp"),
            P("dp", "tp"),
        ),
        out_specs=(P("dp", "tp"), P(("tp", "dp"), None)),
        check_vma=False,
    )
```

profile of v0, /device:TPU:0, one launch (start us, length us, event | category | flops | bytes accessed | tf_op | source)
XLA Modules:
  0.0 160.0 jit_solution(6539963173351391971)
XLA Ops:
  7.2 1.6 copy-done
  8.8 1.4 convolution_bitcast_fusion
  10.4 0.2 reshape.67
  10.6 1.1 fusion.32
  11.7 0.4 multiply_reduce_fusion
  12.1 0.2 copy.12
  12.5 21.3 %all_gather.19 = bf16[96,4096]{1,0:T(8,128)(2,1)S(1)} all-gather(bf16[24,4096]{1,0:T(8,128)(2,1)S(1)} %divide_convert_fusion), channel_id=1, replica_groups=mesh['dp'=8,'tp'=4] {'tp'}, dimensions={0}, use_global_device_ids=true | all-gather | bytes 983040 | tf_op jit(solution)/shard_map/all_gather | solution.py:48
  33.8 5.0 %fusion.35 = f32[96,1024]{1,0:T(8,128)S(1)} fusion(bf16[96,4096]{1,0:T(8,128)(2,1)S(1)} %all_gather.19, bf16[4096,1024]{1,0:T(8,128)(2,1)} %param.12), kind=kOutput, calls=%fused_computation.52 | convolution fusion | flops 805306368 | bytes 9568256 | tf_op jit(solution)/shard_map/dot_general | solution.py:47
  38.8 0.4 convolution_convert_fusion.2
  39.2 0.2 reshape.65
  39.4 0.3 pad_maximum_fusion
  39.7 1.0 copy.11
  40.8 0.7 dynamic-slice
  42.2 0.8 dynamic-update-slice
  43.0 18.0 %reduce-scatter.7.cloned.1.call-done = bf16[384,96]{1,0:T(8,128)(2,1)} async-done(((bf16[1536,96]{1,0:T(8,128)(2,1)}), bf16[384,96]{1,0:T(8,128)(2,1)}) %reduce-scatter.7.cloned.1.call-update) | async-done | bytes 73744
  61.0 1.0 copy.10
  62.4 0.2 dynamic-update-slice.2
  62.6 9.2 %all-reduce.4 = (f32[4]{0:T(128)}, f32[384]{0:T(512)S(1)}, f32[384]{0:T(512)S(1)}) all-reduce(f32[4]{0:T(128)S(1)} %dynamic-update-slice, f32[384]{0:T(512)S(1)} %get-tuple-element.70, f32[384]{0:T(512)S(1)} %dynamic-update-slice.2), channel_id=1, replica_groups=mesh['dp'=8,'tp'=4] {'tp'}, use_global_device_ids=true, to_apply=%add | all-reduce | flops 772 | bytes 6176
  71.9 0.7 slice.24
  72.8 13.8 %while.14 = (s32[]{:T(128)}, f32[]{:T(128)}, f32[96]{0:T(128)S(1)}, f32[96]{0:T(128)S(1)}, f32[3]{0:T(128)S(1)}, /*index=5*/f32[3,96]{1,0:T(4,128)S(1)}, f32[3,96]{1,0:T(4,128)S(1)}, s32[]{:T(128)}) while((s32[]{:T(128)}, f32[]{:T(128)}, f32[96]{0:T(128)S(1)}, f32[96]{0:T(128)S(1)}, f32[3]{0:T(128)S(1)}, /*index=5*/f32[3,96]{1,0:T(4,128)S(1)}, ...), condition=%wide.region_6.7_spmd, body=%wide.region_5.6_spmd.sunk | while | flops 678 | bytes 2469 | solution.py:11
  72.8 0.7 dynamic_slice.32
  77.5 0.7 dynamic_slice.32
  82.1 0.7 dynamic_slice.32
  86.7 0.7 add_rsqrt_fusion
  87.3 0.2 fusion.25
  87.5 10.2 %all-reduce.3 = (f32[96]{0:T(128)S(1)}, f32[96]{0:T(128)S(1)}) all-reduce(f32[96]{0:T(128)S(1)} %get-tuple-element.45, f32[96]{0:T(128)S(1)} %get-tuple-element.44), channel_id=1, replica_groups=mesh['dp'=8,'tp'=4] {'tp'}, use_global_device_ids=true, to_apply=%region_10.11 | all-reduce | flops 192 | bytes 1536 | tf_op jit(solution)/shard_map/psum | solution.py:76
  97.8 0.7 fusion.24
  98.5 14.1 %all_gather.24 = bf16[96,1536]{1,0:T(8,128)(2,1)S(1)} all-gather(bf16[96,384]{1,0:T(8,128)(2,1)S(1)} %get-tuple-element.67), channel_id=1, replica_groups=mesh['dp'=8,'tp'=4] {'tp'}, dimensions={1}, use_global_device_ids=true | all-gather | bytes 368640 | tf_op jit(solution)/shard_map/all_gather | solution.py:84
  112.7 0.2 reshape.69
  112.9 1.8 %convolution_convert_fusion = bf16[1024,768]{1,0:T(8,128)(2,1)} fusion(bf16[96,768]{1,0:T(8,128)(2,1)S(1)} %reshape.69, f32[96,1024]{1,0:T(8,128)S(1)} %fusion.35), kind=kOutput, calls=%fused_computation.8 | convolution fusion | flops 152666112 | bytes 2113536 | tf_op jit(solution)/shard_map/rh,rc->hc/dot_general | solution.py:90
  114.7 36.7 %reduce-scatter.5.cloned.1.call-done = bf16[128,768]{1,0:T(8,128)(2,1)} async-done(((bf16[1024,768]{1,0:T(8,128)(2,1)}), bf16[128,768]{1,0:T(8,128)(2,1)}) %reduce-scatter.5.cloned.1.call-update) | async-done | bytes 196624 | tf_op jit(solution)/shard_map/reduce_scatter | solution.py:89
  151.4 1.7 %convert_element_type.40 = f32[128,768]{1,0:T(8,128)} convert(bf16[128,768]{1,0:T(8,128)(2,1)} %reduce-scatter.5.cloned.1.call-done) | non-fusion elementwise | flops 98304 | bytes 589824 | tf_op jit(solution)/shard_map/convert_element_type | solution.py:96
  (39 shorter events, 1.3 us)
Async XLA Ops:
  7.2 1.7 %copy-start = (bf16[24,192,256]{2,1,0:T(8,128)(2,1)S(1)}, bf16[24,192,256]{2,1,0:T(8,128)(2,1)}, u32[]{:S(2)}) copy-start(bf16[24,192,256]{2,1,0:T(8,128)(2,1)} %param.9) | copy-start | bytes 7077892
  7.2 3.4 %copy-start.2 = (bf16[256,16]{0,1:T(8,128)(2,1)S(1)}, bf16[256,16]{0,1:T(8,128)(2,1)}, u32[]{:S(2)}) copy-start(bf16[256,16]{0,1:T(8,128)(2,1)} %param.10) | copy-start | bytes 24580
  7.2 53.8 %reduce-scatter.7.cloned.1.call-start = ((), (), s32[]{:S(2)}) async-start(), calls=%async_computation.3 | async-start | bytes 491520
  33.8 5.0 %copy-start.4 = (bf16[1024,768]{1,0:T(8,128)(2,1)S(1)}, bf16[1024,768]{1,0:T(8,128)(2,1)}, u32[]{:S(2)}) copy-start(bf16[1024,768]{1,0:T(8,128)(2,1)} %param.13) | copy-start | bytes 4718596
  38.8 2.0 %copy-start.5 = (u32[32]{0:T(128)S(1)}, u32[32]{0:T(128)}, u32[]{:S(2)}) copy-start(u32[32]{0:T(128)} %constant.49) | copy-start | bytes 388
  38.8 48.5 %copy-start.1 = (bf16[96,384]{1,0:T(8,128)(2,1)S(1)}, bf16[96,384]{1,0:T(8,128)(2,1)}, u32[]{:S(2)}) copy-start(bf16[96,384]{1,0:T(8,128)(2,1)} %param.15) | copy-start | bytes 221188
  38.8 48.5 %copy-start.3 = (f32[384]{0:T(512)S(1)}, f32[384]{0:T(512)}, u32[]{:S(2)}) copy-start(f32[384]{0:T(512)} %param.14) | copy-start | bytes 4612
  40.7 110.7 %reduce-scatter.5.cloned.1.call-start = ((), (), s32[]{:S(2)}) async-start(), calls=%async_computation.2 | async-start | bytes 1769472 | tf_op jit(solution)/shard_map/reduce_scatter | solution.py:89
Sparse Core Ops, SparseCore 0:
  40.8 20.1 reduce-scatter.6
  114.9 36.5 reduce-scatter.4
where the time goes:
time: 160 us
  blocking collectives  54.8 us (34%)
  waiting for transfers between devices  54.7 us (34%)
  between operations  14.9 us (9%)
  loops' own time  11.8 us (7%)
  matrix products  9.68 us (6%)
  local copies, waits for them, and re-layouts  9.47 us (6%)
  other arithmetic  4.5 us (3%)
    reduce_scatter x1, waiting for transfers between devices, on_device(): lax.psum_scatter(jnp.einsum('rh,rc->hc', hidden, mlp_grad, preferred_elem...  36.7 us
    all_gather x1, blocking collectives, on_device(): lax.all_gather(normed, 'tp', axis=0, tiled=True)  21.3 us
    unnamed x3, waiting for transfers between devices  18.1 us
    all_gather x1, blocking collectives, on_device(): mixed_gradient = lax.all_gather(local_grad, 'tp', axis=1, tiled=True)  14.1 us
    another operation x1, loops' own time, merged(): lax.scan(lambda subtotal, share: (join(subtotal, share), None), head, tail)  11.8 us
    psum x1, blocking collectives, on_device(): lax.psum((jnp.sum(scaled_rows, axis=1), jnp.sum(scaled_rows * centered_ro...  10.2 us
    unnamed x1, blocking collectives  9.16 us
    unnamed x21, local copies, waits for them, and re-layouts  5.57 us
  transfers between devices with their start and end apart: 2, of which 2 were waited for; matrix products, arithmetic and copies ran while one was open for 1% of the time, Pallas kernels for 0%

commit v1 on v0

--- a/solution.py
+++ b/solution.py
@@ -1,7 +1,356 @@
+import functools
+
 import jax
 import jax.numpy as jnp
 from jax import lax
+from jax.experimental import pallas as pl
+from jax.experimental.pallas import tpu as pltpu
 from jax.sharding import PartitionSpec as P
+
+CHUNKS = 4
+EPS = 1e-05
+
+
+def fused_kernel(
+    dp, tp, samples, rows, group,
+    norm_ref, lcb_ref, up_hbm, down_hbm, gain_ref, cot_ref,
+    res_ref, grad_ref,
+    up, down, gathered, lcb_in, acc, hid, hid_in, part, part_in, stat, stat_in, dmix, half_out, half_in,
+    load_sem, ag_send, ag_recv, lcb_send, lcb_recv, hid_send, hid_recv, part_send, part_recv,
+    stat_send, stat_recv, col_send, col_recv, x_send, x_recv, y_send, y_recv, d_send, d_recv, c_send, c_recv,
+):
+    me = lax.axis_index("tp")
+    ring = lax.axis_index("dp")
+    core = lax.rem(ring, 2)
+    east = lax.rem(ring // 2, 2)
+    north = ring // 4
+    x_peer = ring + 2 - 4 * east
+    y_peer = ring + 4 - 8 * north
+    d_peer = x_peer + 4 - 8 * north
+    c_peer = ring + 1 - 2 * core
+    chip = ring // 2
+    half = rows // 2
+    tall = 2 * samples
+    feats = norm_ref.shape[2]
+    width = 2 * group
+
+    loads = []
+    for c in range(CHUNKS):
+        piece = pl.ds(c * 2 * feats, 2 * feats)
+        loads.append(pltpu.make_async_copy(up_hbm.at[piece], up.at[piece], load_sem.at[c]))
+    loads.append(pltpu.make_async_copy(down_hbm, down, load_sem.at[CHUNKS]))
+    for load in loads:
+        load.start()
+
+    peers = [{"tp": lax.rem(me + k, tp)} for k in range(1, tp)]
+    others = [{"dp": x_peer}, {"dp": y_peer}, {"dp": d_peer}, {"dp": c_peer}]
+    barrier = pltpu.get_barrier_semaphore()
+    for peer in peers + others:
+        pl.semaphore_signal(barrier, inc=1, device_id=peer, device_id_type=pl.DeviceIdType.MESH)
+    pl.semaphore_wait(barrier, tp + 3)
+
+    def remote(src, dst, send, recv, peer):
+        return pltpu.make_async_remote_copy(
+            src_ref=src, dst_ref=dst, send_sem=send, recv_sem=recv,
+            device_id=peer, device_id_type=pl.DeviceIdType.MESH,
+        )
+
+    def block_rows(owner):
+        return pl.ds(pl.multiple_of(owner * tall, tall), tall)
+
+    def hop(way, d, c):
+        step = 1 if way == 0 else -1
+        owner = me - step * d
+        dst = gathered.at[c, block_rows(owner)]
+        src = norm_ref.at[c] if d == 0 else dst
+        return remote(src, dst, ag_send.at[way, d, c], ag_recv.at[way, d + 1, c],
+                      {"tp": lax.rem(me + step + tp, tp)})
+
+    def arrival(way, d, c):
+        step = 1 if way == 0 else -1
+        owner = me - step * d
+        dst = gathered.at[c, block_rows(owner)]
+        return remote(dst, dst, ag_send.at[way, d, c], ag_recv.at[way, d, c],
+                      {"tp": lax.rem(me + step + tp, tp)})
+
+    def sends(way, d):
+        return (me >= d) & (me < tp - 1) if way == 0 else (me < tp - d) & (me > 0)
+
+    def gets(way, d):
+        return me >= d if way == 0 else me < tp - d
+
+    for way in range(2):
+        @pl.when(sends(way, 0))
+        def _():
+            for c in range(CHUNKS):
+                hop(way, 0, c).start()
+    for c in range(CHUNKS):
+        gathered[c, block_rows(me)] = norm_ref[c]
+    lcb_in[me] = lcb_ref[me]
+
+    def lcb_copy(k):
+        return remote(lcb_ref.at[lax.rem(me + k, tp)], lcb_in.at[me], lcb_send.at[k], lcb_recv.at[k], peers[k - 1])
+
+    def lcb_arrival(k):
+        src = lax.rem(me - k + tp, tp)
+        return remote(lcb_in.at[src], lcb_in.at[src], lcb_send.at[k], lcb_recv.at[k], peers[k - 1])
+
+    for d in range(1, tp):
+        if d == tp - 1:
+            for k in range(1, tp):
+                lcb_copy(k).start()
+        for c in range(CHUNKS):
+            for way in range(2):
+                @pl.when(gets(way, d))
+                def _():
+                    arrival(way, d, c).wait_recv()
+                if d < tp - 1:
+                    @pl.when(sends(way, d))
+                    def _():
+                        hop(way, d, c).start()
+            if d == tp - 1:
+                loads[c].wait()
+                for side in range(2):
+                    term = jnp.dot(gathered[c], up[pl.ds((2 * c + side) * feats, feats), :],
+                                   preferred_element_type=jnp.float32)
+                    if c == 0:
+                        acc[side] = term
+                    else:
+                        acc[side] += term
+
+    for t in range(tp):
+        total = acc[0, t * tall:t * tall + samples] + acc[1, t * tall + samples:(t + 1) * tall]
+        acc[0, t * samples:(t + 1) * samples] = total
+    chips = dp // 2
+    span = hid.shape[2]
+    for q in range(chips):
+        hid[q] = jax.nn.gelu(acc[0, :rows, q * span:(q + 1) * span], approximate=True).astype(jnp.bfloat16)
+
+    def hid_copy(slot, peer):
+        return remote(hid.at[peer // 2], hid_in.at[slot], hid_send.at[slot], hid_recv.at[slot], {"dp": peer})
+
+    hid_copies = [hid_copy(1, x_peer), hid_copy(2, y_peer), hid_copy(3, d_peer)]
+    for copy in hid_copies:
+        copy.start()
+    hid_in[0] = hid[chip]
+
+    loads[CHUNKS].wait()
+    mlp = jnp.dot(hid[0], down[0:span, :], preferred_element_type=jnp.float32)
+    for q in range(1, chips):
+        mlp += jnp.dot(hid[q], down[q * span:(q + 1) * span, :], preferred_element_type=jnp.float32)
+    for g in range(tp):
+        piece = mlp[:, g * group:(g + 1) * group]
+        part[g] = jnp.concatenate([piece[:half], piece[half:]], axis=1).astype(jnp.bfloat16)
+    part_copies = [
+        remote(part.at[lax.rem(me + k, tp)], part_in.at[k], part_send.at[k], part_recv.at[k], peers[k - 1])
+        for k in range(1, tp)
+    ]
+    for copy in part_copies:
+        copy.start()
+
+    gain = gain_ref[...]
+    gg = cot_ref[...].astype(jnp.float32) * gain
+    for k in range(1, tp):
+        lcb_arrival(k).wait_recv()
+    packed = part[me].astype(jnp.float32)
+    for k in range(1, tp):
+        part_copies[k - 1].wait_recv()
+        packed += part_in[k].astype(jnp.float32)
+    summed = jnp.concatenate([packed[:, :group], packed[:, group:]], axis=0)
+    linear = jnp.concatenate([lcb_in[t] for t in range(tp)], axis=0)
+    mix = jnp.concatenate([summed, linear], axis=1)
+
+    mean = jnp.sum(mix, axis=1, keepdims=True) * (1.0 / width)
+    off = mix - mean
+    dev = jnp.sum(off * off, axis=1, keepdims=True)
+    first = jnp.sum(gg, axis=1, keepdims=True)
+    second = jnp.sum(gg * off, axis=1, keepdims=True)
+    lane = lax.broadcasted_iota(jnp.int32, (rows, 128), 1)
+    table = jnp.where(lane == 0, mean, jnp.where(lane == 1, dev, jnp.where(lane == 2, first, second)))
+    if rows < 128:
+        table = jnp.concatenate([table, jnp.zeros((128 - rows, 128), jnp.float32)], axis=0)
+    stat[...] = table.T[:8]
+    stat_copies = [
+        remote(stat, stat_in.at[k], stat_send.at[k], stat_recv.at[k], peers[k - 1]) for k in range(1, tp)
+    ]
+    for copy in stat_copies:
+        copy.start()
+    tables = [stat[...]]
+    for k in range(1, tp):
+        stat_copies[k - 1].wait_recv()
+        tables.append(stat_in[k])
+    full = float(tp * width)
+    mean_all = sum(t[0:1] for t in tables) * (1.0 / tp)
+    dev_all = sum(t[1:2] + (t[0:1] - mean_all) * (t[0:1] - mean_all) * float(width) for t in tables)
+    first_all = sum(t[2:3] for t in tables) * (1.0 / full)
+    rstd_all = 1.0 / jnp.sqrt(dev_all * (1.0 / full) + EPS)
+    second_all = sum(t[3:4] + (t[0:1] - mean_all) * t[2:3] for t in tables) * rstd_all * (1.0 / full)
+    back = jnp.concatenate(
+        [mean_all, rstd_all, first_all, second_all, jnp.zeros((124, 128), jnp.float32)], axis=0
+    ).T[:rows]
+    mean_c, rstd_c, first_c, second_c = back[:, 0:1], back[:, 1:2], back[:, 2:3], back[:, 3:4]
+    xhat = (mix - mean_c) * rstd_c
+    grad = (gg[:, :group] - first_c - xhat[:, :group] * second_c) * rstd_c
+    dmix[0, me] = jnp.concatenate([grad[:half], grad[half:]], axis=1).astype(jnp.bfloat16)
+
+    def owner_at(k):
+        return lax.rem(me + k, tp)
+
+    def col_copy(k):
+        return remote(dmix.at[0, me], dmix.at[0, me], col_send.at[k], col_recv.at[k], peers[k - 1])
+
+    def col_arrival(k):
+        ref = dmix.at[0, owner_at(k)]
+        return remote(ref, ref, col_send.at[tp - k], col_recv.at[tp - k], peers[k - 1])
+
+    def x_copy(k):
+        return remote(dmix.at[0, owner_at(k)], dmix.at[1, owner_at(k)], x_send.at[k], x_recv.at[k], {"dp": x_peer})
+
+    def y_copy(k):
+        return remote(dmix.at[0, owner_at(k)], dmix.at[2, owner_at(k)], y_send.at[k], y_recv.at[k], {"dp": y_peer})
+
+    def x_arrival(k):
+        return remote(dmix.at[0, owner_at(k)], dmix.at[1, owner_at(k)], x_send.at[k], x_recv.at[k], {"dp": x_peer})
+
+    def y_arrival(k):
+        return remote(dmix.at[0, owner_at(k)], dmix.at[2, owner_at(k)], y_send.at[k], y_recv.at[k], {"dp": y_peer})
+
+    def d_copy(k):
+        slot, peer = (1, y_peer) if k % 2 == 0 else (2, x_peer)
+        return remote(dmix.at[slot, owner_at(k)], dmix.at[3, owner_at(k)], d_send.at[k], d_recv.at[k], {"dp": peer})
+
+    for k in range(1, tp):
+        col_copy(k).start()
+    x_copy(0).start()
+    y_copy(0).start()
+    res_ref[...] = (xhat * gain).astype(jnp.bfloat16)
+    for copy in hid_copies:
+        copy.wait_recv()
+    for k in range(tp + 1):
+        if 0 < k < tp:
+            col_arrival(k).wait_recv()
+            x_copy(k).start()
+            y_copy(k).start()
+        if k > 0:
+            x_arrival(k - 1).wait_recv()
+            y_arrival(k - 1).wait_recv()
+            d_copy(k - 1).start()
+    for k in range(tp):
+        d_copy(k).wait_recv()
+
+    across = (((0,), (0,)), ((), ()))
+    low = jnp.concatenate([hid_in[s, :half] for s in range(chips)], axis=0)
+    high = jnp.concatenate([hid_in[s, half:] for s in range(chips)], axis=0)
+    columns = []
+    for g in range(tp):
+        block = jnp.concatenate([dmix[s, g] for s in range(chips)], axis=0)
+        left = lax.dot_general(low, block, across, preferred_element_type=jnp.float32)
+        right = lax.dot_general(high, block, across, preferred_element_type=jnp.float32)
+        columns.append(left[:, :group] + right[:, group:])
+    result = jnp.concatenate(columns, axis=1)
+    mine = span // 2
+    own = jnp.where(core == 0, result[:mine], result[mine:])
+    half_out[...] = jnp.where(core == 0, result[mine:], result[:mine]).astype(jnp.bfloat16)
+    c_copy = remote(half_out, half_in, c_send, c_recv, {"dp": c_peer})
+    c_copy.start()
+
+    for way in range(2):
+        for d in range(tp - 1):
+            @pl.when(sends(way, d))
+            def _():
+                for c in range(CHUNKS):
+                    hop(way, d, c).wait_send()
+    for copy in hid_copies + part_copies + stat_copies:
+        copy.wait_send()
+    for k in range(1, tp):
+        lcb_copy(k).wait_send()
+        col_copy(k).wait_send()
+    for k in range(tp):
+        x_copy(k).wait_send()
+        y_copy(k).wait_send()
+        d_copy(k).wait_send()
+    c_copy.wait()
+    grad_ref[...] = own + half_in[...].astype(jnp.float32)
+
+
+def fused_device(dp, tp, embeddings, projection, compress, w_up, w_down, output_norm_gain, out_grad):
+    samples = embeddings.shape[0]
+    rows = samples * tp
+    group = w_down.shape[1] // tp
+    hidden = w_up.shape[1]
+    pairs = jnp.einsum(
+        "sef,fk->sek", embeddings, projection, preferred_element_type=jnp.float32
+    ).astype(jnp.bfloat16)
+    inter = jnp.einsum(
+        "sek,sef->skf", pairs, embeddings, preferred_element_type=jnp.float32
+    )
+    center = inter - jnp.mean(inter, axis=(1, 2), keepdims=True)
+    spread = jnp.mean(center * center, axis=(1, 2), keepdims=True)
+    normed = (center / jnp.sqrt(spread + EPS)).astype(jnp.bfloat16)
+    lcb = jnp.einsum(
+        "sef,fj->sje", embeddings, compress, preferred_element_type=jnp.float32
+    ).reshape(samples, tp, group).transpose(1, 0, 2)
+    feats = w_up.shape[0] // (2 * CHUNKS)
+    normed = normed.reshape(samples, CHUNKS, 2, feats).transpose(1, 2, 0, 3).reshape(CHUNKS, 2 * samples, feats)
+    span = 2 * hidden // dp
+    chips = dp // 2
+    half = rows // 2
+    width = 2 * group
+    bf16, f32, dma = jnp.bfloat16, jnp.float32, pltpu.SemaphoreType.DMA
+    vmem = pl.BlockSpec(memory_space=pltpu.VMEM)
+    hbm = pl.BlockSpec(memory_space=pl.ANY)
+    return pl.pallas_call(
+        functools.partial(fused_kernel, dp, tp, samples, rows, group),
+        out_shape=(
+            jax.ShapeDtypeStruct((rows, width), bf16),
+            jax.ShapeDtypeStruct((span // 2, w_down.shape[1]), f32),
+        ),
+        in_specs=[vmem, vmem, hbm, hbm, vmem, vmem],
+        out_specs=(vmem, vmem),
+        scratch_shapes=[
+            pltpu.VMEM(w_up.shape, bf16),
+            pltpu.VMEM(w_down.shape, bf16),
+            pltpu.VMEM((CHUNKS, tp * 2 * samples, feats), bf16),
+            pltpu.VMEM((tp, samples, group), f32),
+            pltpu.VMEM((2, tp * 2 * samples, hidden), f32),
+            pltpu.VMEM((chips, rows, span), bf16),
+            pltpu.VMEM((chips, rows, span), bf16),
+            pltpu.VMEM((tp, half, width), bf16),
+            pltpu.VMEM((tp, half, width), bf16),
+            pltpu.VMEM((8, 128), f32),
+            pltpu.VMEM((tp, 8, 128), f32),
+            pltpu.VMEM((chips, tp, half, width), bf16),
+            pltpu.VMEM((span // 2, w_down.shape[1]), bf16),
+            pltpu.VMEM((span // 2, w_down.shape[1]), bf16),
+            dma((CHUNKS + 1,)),
+            dma((2, tp, CHUNKS)), dma((2, tp, CHUNKS)),
+            dma((tp,)), dma((tp,)),
+            dma((4,)), dma((4,)),
+            dma((tp,)), dma((tp,)),
+            dma((tp,)), dma((tp,)),
+            dma((tp,)), dma((tp,)),
+            dma((tp,)), dma((tp,)),
+            dma((tp,)), dma((tp,)),
+            dma((tp,)), dma((tp,)),
+            dma, dma,
+        ],
+        compiler_params=pltpu.CompilerParams(
+            collective_id=0, has_side_effects=True, vmem_limit_bytes=48 * 1024 * 1024
+        ),
+        name="block",
+    )(normed, lcb, w_up, w_down, output_norm_gain.reshape(1, width), out_grad)
+
+
+def fits(dp, tp, args):
+    embeddings, w_up, w_down = args[0], args[3], args[4]
+    if dp != 8 or tp < 2 or embeddings.shape[0] % (dp * tp):
+        return False
+    samples = embeddings.shape[0] // (dp * tp)
+    rows, group, hidden = samples * tp, w_down.shape[1] // tp, w_up.shape[1] // tp
+    return (
+        samples % 8 == 0 and rows % 32 == 0 and rows <= 128 and group % 64 == 0
+        and hidden % (128 * dp) == 0 and w_up.shape[0] % (256 * CHUNKS) == 0
+    )
 
 
 def merged(value, axis, join):
@@ -98,18 +447,24 @@
 
 
 def solution(mesh):
-    return jax.shard_map(
-        on_device,
-        mesh=mesh,
-        in_specs=(
-            P(("dp", "tp"), None, None),
-            P(),
-            P(),
-            P(None, "tp"),
-            P("tp", None),
-            P("tp"),
-            P("dp", "tp"),
-        ),
-        out_specs=(P("dp", "tp"), P(("tp", "dp"), None)),
-        check_vma=False,
-    )
+    dp, tp = mesh.shape["dp"], mesh.shape["tp"]
+
+    def whole(*args):
+        body = functools.partial(fused_device, dp, tp) if fits(dp, tp, args) else on_device
+        return jax.shard_map(
+            body,
+            mesh=mesh,
+            in_specs=(
+                P(("dp", "tp"), None, None),
+                P(),
+                P(),
+                P(None, "tp"),
+                P("tp", None),
+                P("tp"),
+                P("dp", "tp"),
+            ),
+            out_specs=(P("dp", "tp"), P(("tp", "dp"), None)),
+            check_vma=False,
+        )(*args)
+
+    return whole

time: 160 us -> 56 us (0.35)
  blocking collectives: 54.8 us -> 0 us
  waiting for transfers between devices: 54.7 us -> 0 us
  Pallas kernels: 0 us -> 47.3 us
  between operations: 14.9 us -> 0.72 us
  loops' own time: 11.8 us -> 0 us
  matrix products: 9.68 us -> 2.52 us
  local copies, waits for them, and re-layouts: 9.47 us -> 4.69 us
  other arithmetic: 4.5 us -> 0.55 us
    pallas_call x0 -> x1, Pallas kernels: none -> 47.3 us  [fused_device(): pl.pallas_call(functools.partial(fused_kernel, dp, tp, samples, rows, gro...]
    reduce_scatter x1 -> x0, waiting for transfers between devices: 36.7 us -> none  [on_device(): lax.psum_scatter(jnp.einsum('rh,rc->hc', hidden, mlp_grad, preferred_elem...]
    all_gather x2 -> x0, blocking collectives: 35.4 us -> none  [the longest x1 21.3 us: on_device(): lax.all_gather(normed, 'tp', axis=0, tiled=True)]
    unnamed x3 -> x0, waiting for transfers between devices: 18.1 us -> none
    another operation x1 -> x0, loops' own time: 11.8 us -> none  [merged(): lax.scan(lambda subtotal, share: (join(subtotal, share), None), head, tail)]
    psum x1 -> x0, blocking collectives: 10.2 us -> none  [on_device(): lax.psum((jnp.sum(scaled_rows, axis=1), jnp.sum(scaled_rows * centered_ro...]
    unnamed x1 -> x0, blocking collectives: 9.16 us -> none
    dot_general x5 -> x2, matrix products: 9.68 us -> 2.52 us  [the longest x1 1.38 us: fused_device(): jnp.einsum('sef,fj->sje', embeddings, compress, preferred_element_type=jn...]
  transfers between devices with their start and end apart: 2 -> 0, of which waited for: 2 -> 0; matrix products, arithmetic and copies ran while one was open for 1% -> 0% of each run, Pallas kernels for 0% -> 0%
where the time goes in v1:
time: 56 us; the launch traced here: 55.8 us
  Pallas kernels  47.3 us (84%)
  local copies, waits for them, and re-layouts  4.69 us (8%)
  matrix products  2.52 us (4%)
  between operations  0.72 us (1%)
    pallas_call x1, Pallas kernels, fused_device(): pl.pallas_call(functools.partial(fused_kernel, dp, tp, samples, rows, gro...  47.3 us
    unnamed x10, local copies, waits for them, and re-layouts  3.63 us
    dot_general x1, matrix products, fused_device(): jnp.einsum('sef,fj->sje', embeddings, compress, preferred_element_type=jn...  1.38 us
    dot_general x1, matrix products, fused_device(): jnp.einsum('sek,sef->skf', pairs, embeddings, preferred_element_type=jnp....  1.14 us

profile of v1, /device:TPU:0, one launch (start us, length us, event | category | flops | bytes accessed | tf_op | source)
XLA Modules:
  0.0 55.8 jit_solution(13017890937256100295)
XLA Ops:
  0.6 0.0 copy-start
  0.6 0.0 copy-start.3
  0.7 0.8 %reshape.27.gain_ref = f32[1,384]{1,0:T(1,128)S(1)} reshape(f32[384]{0:T(512)} %param.12) | data formatting | bytes 3072 | tf_op jit(solution)/shard_map/reshape | solution.py:341
  1.5 0.8 %copy-done = bf16[24,192,256]{2,1,0:T(8,128)(2,1)S(1)} copy-done((bf16[24,192,256]{2,1,0:T(8,128)(2,1)S(1)}, bf16[24,192,256]{2,1,0:T(8,128)(2,1)}, u32[]{:S(2)}) %copy-start) | copy-done | bytes 2359320
  2.3 1.4 %fusion.3 = f32[4,24,192]{2,0,1:T(4,128)S(1)} fusion(bf16[24,192,256]{2,1,0:T(8,128)(2,1)S(1)} %copy-done, bf16[256,4]{0,1:T(4,128)(2,1)} %param.9), kind=kOutput, calls=%fused_computation.5 | convolution fusion | flops 9437184 | bytes 2435072 | tf_op jit(solution)/shard_map/sef,fj->sje/dot_general | solution.py:290
  3.7 0.0 copy-done.3
  3.8 0.0 copy-start.2
  3.8 1.1 %fusion.5 = (f32[24]{0:T(128)S(1)}, f32[24,16,256]{2,1,0:T(8,128)S(1)}) fusion(bf16[24,192,256]{2,1,0:T(8,128)(2,1)S(1)} %copy-done, bf16[256,16]{0,1:T(8,128)(2,1)S(1)} %copy-done.3), kind=kOutput, calls=%fused_computation.9 | convolution fusion | flops 75669480 | bytes 2760800 | tf_op jit(solution)/shard_map/sek,sef->skf/dot_general | solution.py:284
  4.9 0.4 multiply_reduce_fusion
  5.3 0.1 divide_convert_fusion
  5.5 0.1 reshape.25
  5.6 0.1 copy.9
  5.7 0.0 copy-done.2
  5.7 0.0 copy-start.1
  5.7 1.4 %copy-done.1 = bf16[1024,768]{1,0:T(8,128)(2,1)S(1)} copy-done((bf16[1024,768]{1,0:T(8,128)(2,1)S(1)}, bf16[1024,768]{1,0:T(8,128)(2,1)}, u32[]{:S(2)}) %copy-start.1) | copy-done | bytes 1572888
  7.1 47.3 %block.1 = (bf16[96,384]{1,0:T(8,128)(2,1)S(1)}, f32[128,768]{1,0:T(8,128)S(1)}) custom-call(bf16[4,48,512]{2,1,0:T(8,128)(2,1)S(1)} %bitcast.15, f32[4,24,192]{2,1,0:T(8,128)S(1)} %copy.10.lcb_ref, bf16[4096,1024]{1,0:T(8,128)(2,1)} %up_hbm.1, bf16[1024,768]{1,0:T(8,128)(2,1)S(1)} %copy-done.1, f32[1,384]{1,0:T(1,128)S(1)} %reshape.27.gain_ref, ...), custom_call_target="tpu_custom_call" | custom-call | tf_op jit(solution)/shard_map/block/pallas_call | solution.py:302
  54.4 0.6 %copy.13 = bf16[96,384]{1,0:T(8,128)(2,1)} copy(bf16[96,384]{1,0:T(8,128)(2,1)S(1)} %get-tuple-element.6) | data formatting | bytes 147456
  55.0 0.7 %copy.14 = f32[128,768]{1,0:T(8,128)} copy(f32[128,768]{1,0:T(8,128)S(1)} %get-tuple-element.7) | data formatting | bytes 786432
  (3 shorter events, 0.1 us)
Async XLA Ops:
  0.6 1.7 %copy-start = (bf16[24,192,256]{2,1,0:T(8,128)(2,1)S(1)}, bf16[24,192,256]{2,1,0:T(8,128)(2,1)}, u32[]{:S(2)}) copy-start(bf16[24,192,256]{2,1,0:T(8,128)(2,1)} %param.7) | copy-start | bytes 7077892
  0.6 3.1 %copy-start.3 = (bf16[256,16]{0,1:T(8,128)(2,1)S(1)}, bf16[256,16]{0,1:T(8,128)(2,1)}, u32[]{:S(2)}) copy-start(bf16[256,16]{0,1:T(8,128)(2,1)} %param.8) | copy-start | bytes 24580
  3.8 1.9 %copy-start.2 = (bf16[96,384]{1,0:T(8,128)(2,1)S(1)}, bf16[96,384]{1,0:T(8,128)(2,1)}, u32[]{:S(2)}) copy-start(bf16[96,384]{1,0:T(8,128)(2,1)} %cot_ref.1) | copy-start | bytes 221188
  5.7 1.4 %copy-start.1 = (bf16[1024,768]{1,0:T(8,128)(2,1)S(1)}, bf16[1024,768]{1,0:T(8,128)(2,1)}, u32[]{:S(2)}) copy-start(bf16[1024,768]{1,0:T(8,128)(2,1)} %down_hbm.1) | copy-start | bytes 4718596

commit v2 on v1

--- a/solution.py
+++ b/solution.py
@@ -13,10 +13,10 @@
 
 def fused_kernel(
     dp, tp, samples, rows, group,
-    norm_ref, lcb_ref, up_hbm, down_hbm, gain_ref, cot_ref,
+    emb_hbm, proj_ref, comp_ref, up_hbm, down_hbm, gain_ref, cot_ref,
     res_ref, grad_ref,
-    up, down, gathered, lcb_in, acc, hid, hid_in, part, part_in, stat, stat_in, dmix, half_out, half_in,
-    load_sem, ag_send, ag_recv, lcb_send, lcb_recv, hid_send, hid_recv, part_send, part_recv,
+    emb, inter, linear_rows, lcb_ref, up, down, gathered, lcb_in, acc, hid, hid_in, part, part_in, stat, stat_in, dmix, half_out, half_in,
+    emb_sem, load_sem, ag_send, ag_recv, lcb_send, lcb_recv, hid_send, hid_recv, part_send, part_recv,
     stat_send, stat_recv, col_send, col_recv, x_send, x_recv, y_send, y_recv, d_send, d_recv, c_send, c_recv,
 ):
     me = lax.axis_index("tp")
@@ -31,9 +31,18 @@
     chip = ring // 2
     half = rows // 2
     tall = 2 * samples
-    feats = norm_ref.shape[2]
+    feats = gathered.shape[2]
+    rank, fields = proj_ref.shape
     width = 2 * group
 
+    batch = emb_sem.shape[0]
+    step = samples // batch
+    emb_loads = [
+        pltpu.make_async_copy(emb_hbm.at[pl.ds(b * step, step)], emb.at[pl.ds(b * step, step)], emb_sem.at[b])
+        for b in range(batch)
+    ]
+    for load in emb_loads:
+        load.start()
     loads = []
     for c in range(CHUNKS):
         piece = pl.ds(c * 2 * feats, 2 * feats)
@@ -42,11 +51,50 @@
     for load in loads:
         load.start()
 
-    peers = [{"tp": lax.rem(me + k, tp)} for k in range(1, tp)]
+    order = [me]
+    for k in range(1, tp):
+        place = me * 0
+        for t in range(tp):
+            near = sorted(range(tp), key=lambda other: (abs(other - t), other))
+            place = place + jnp.where(me == t, near[k], 0)
+        order.append(place)
+    peers = [{"tp": place} for place in order[1:]]
     others = [{"dp": x_peer}, {"dp": y_peer}, {"dp": d_peer}, {"dp": c_peer}]
     barrier = pltpu.get_barrier_semaphore()
     for peer in peers + others:
         pl.semaphore_signal(barrier, inc=1, device_id=peer, device_id_type=pl.DeviceIdType.MESH)
+
+    spare = (-(rank + tp)) % 16
+    strips = [(at, min(at + 128, group)) for at in range(0, group, 128)]
+    head = jnp.concatenate(
+        [proj_ref[...].astype(jnp.float32), comp_ref[...].astype(jnp.float32), jnp.zeros((spare, fields), jnp.float32)],
+        axis=0,
+    ).astype(jnp.bfloat16)
+    for s in range(samples):
+        if s % step == 0:
+            emb_loads[s // step].wait()
+        first = lax.dot_general(head, emb[s], (((1,), (1,)), ((), ())), preferred_element_type=jnp.float32)
+        second = jnp.dot(first[:rank].astype(jnp.bfloat16), emb[s], preferred_element_type=jnp.float32)
+        for h in range(fields // 128):
+            inter[h, s * rank:(s + 1) * rank, :] = second[:, h * 128:(h + 1) * 128]
+        for h, (at, end) in enumerate(strips):
+            linear_rows[h, s * 8:(s + 1) * 8, 0:end - at] = first[rank:rank + 8, at:end]
+    ranks = [
+        jnp.concatenate([inter[h, pl.ds(k, samples, stride=rank), :] for h in range(fields // 128)], axis=1)
+        for k in range(rank)
+    ]
+    count = float(rank * fields)
+    center = jnp.sum(sum(ranks), axis=1, keepdims=True) * (1.0 / count)
+    ranks = [value - center for value in ranks]
+    spread = jnp.sum(sum(value * value for value in ranks), axis=1, keepdims=True) * (1.0 / count)
+    scale = 1.0 / jnp.sqrt(spread + EPS)
+    side_ranks = feats // fields
+    for c in range(CHUNKS):
+        for r in range(side_ranks):
+            top = ranks[2 * c * side_ranks + r] * scale
+            low = ranks[(2 * c + 1) * side_ranks + r] * scale
+            gathered[c, pl.ds(pl.multiple_of(me * tall, tall), tall), r * fields:(r + 1) * fields] = (
+                jnp.concatenate([top, low], axis=0).astype(jnp.bfloat16))
     pl.semaphore_wait(barrier, tp + 3)
 
     def remote(src, dst, send, recv, peer):
@@ -62,8 +110,7 @@
         step = 1 if way == 0 else -1
         owner = me - step * d
         dst = gathered.at[c, block_rows(owner)]
-        src = norm_ref.at[c] if d == 0 else dst
-        return remote(src, dst, ag_send.at[way, d, c], ag_recv.at[way, d + 1, c],
+        return remote(dst, dst, ag_send.at[way, d, c], ag_recv.at[way, d + 1, c],
                       {"tp": lax.rem(me + step + tp, tp)})
 
     def arrival(way, d, c):
@@ -84,16 +131,17 @@
         def _():
             for c in range(CHUNKS):
                 hop(way, 0, c).start()
-    for c in range(CHUNKS):
-        gathered[c, block_rows(me)] = norm_ref[c]
+    for j in range(tp):
+        for h, (at, end) in enumerate(strips):
+            lcb_ref[j, :, at:end] = linear_rows[h, pl.ds(j, samples, stride=8), :][:, :end - at]
     lcb_in[me] = lcb_ref[me]
 
     def lcb_copy(k):
-        return remote(lcb_ref.at[lax.rem(me + k, tp)], lcb_in.at[me], lcb_send.at[k], lcb_recv.at[k], peers[k - 1])
+        return remote(lcb_ref.at[order[k]], lcb_in.at[me], lcb_send.at[k], lcb_recv.at[me], peers[k - 1])
 
     def lcb_arrival(k):
-        src = lax.rem(me - k + tp, tp)
-        return remote(lcb_in.at[src], lcb_in.at[src], lcb_send.at[k], lcb_recv.at[k], peers[k - 1])
+        src = order[k]
+        return remote(lcb_in.at[src], lcb_in.at[src], lcb_send.at[k], lcb_recv.at[src], peers[k - 1])
 
     for d in range(1, tp):
         if d == tp - 1:
@@ -141,12 +189,17 @@
     for g in range(tp):
         piece = mlp[:, g * group:(g + 1) * group]
         part[g] = jnp.concatenate([piece[:half], piece[half:]], axis=1).astype(jnp.bfloat16)
-    part_copies = [
-        remote(part.at[lax.rem(me + k, tp)], part_in.at[k], part_send.at[k], part_recv.at[k], peers[k - 1])
-        for k in range(1, tp)
-    ]
-    for copy in part_copies:
-        copy.start()
+    def exchange(source, landing, send, recv):
+        outs = [remote(source(order[k]), landing.at[me], send.at[k], recv.at[me], peers[k - 1]) for k in range(1, tp)]
+        ins = [
+            remote(landing.at[order[k]], landing.at[order[k]], send.at[k], recv.at[order[k]], peers[k - 1])
+            for k in range(1, tp)
+        ]
+        for copy in reversed(outs):
+            copy.start()
+        return outs, ins
+
+    part_copies, part_ins = exchange(lambda place: part.at[place], part_in, part_send, part_recv)
 
     gain = gain_ref[...]
     gg = cot_ref[...].astype(jnp.float32) * gain
@@ -154,8 +207,8 @@
         lcb_arrival(k).wait_recv()
     packed = part[me].astype(jnp.float32)
     for k in range(1, tp):
-        part_copies[k - 1].wait_recv()
-        packed += part_in[k].astype(jnp.float32)
+        part_ins[k - 1].wait_recv()
+        packed += part_in[order[k]].astype(jnp.float32)
     summed = jnp.concatenate([packed[:, :group], packed[:, group:]], axis=0)
     linear = jnp.concatenate([lcb_in[t] for t in range(tp)], axis=0)
     mix = jnp.concatenate([summed, linear], axis=1)
@@ -170,15 +223,11 @@
     if rows < 128:
         table = jnp.concatenate([table, jnp.zeros((128 - rows, 128), jnp.float32)], axis=0)
     stat[...] = table.T[:8]
-    stat_copies = [
-        remote(stat, stat_in.at[k], stat_send.at[k], stat_recv.at[k], peers[k - 1]) for k in range(1, tp)
-    ]
-    for copy in stat_copies:
-        copy.start()
+    stat_copies, stat_ins = exchange(lambda place: stat, stat_in, stat_send, stat_recv)
     tables = [stat[...]]
     for k in range(1, tp):
-        stat_copies[k - 1].wait_recv()
-        tables.append(stat_in[k])
+        stat_ins[k - 1].wait_recv()
+        tables.append(stat_in[order[k]])
     full = float(tp * width)
     mean_all = sum(t[0:1] for t in tables) * (1.0 / tp)
     dev_all = sum(t[1:2] + (t[0:1] - mean_all) * (t[0:1] - mean_all) * float(width) for t in tables)
@@ -194,14 +243,7 @@
     dmix[0, me] = jnp.concatenate([grad[:half], grad[half:]], axis=1).astype(jnp.bfloat16)
 
     def owner_at(k):
-        return lax.rem(me + k, tp)
-
-    def col_copy(k):
-        return remote(dmix.at[0, me], dmix.at[0, me], col_send.at[k], col_recv.at[k], peers[k - 1])
-
-    def col_arrival(k):
-        ref = dmix.at[0, owner_at(k)]
-        return remote(ref, ref, col_send.at[tp - k], col_recv.at[tp - k], peers[k - 1])
+        return order[k]
 
     def x_copy(k):
         return remote(dmix.at[0, owner_at(k)], dmix.at[1, owner_at(k)], x_send.at[k], x_recv.at[k], {"dp": x_peer})
@@ -219,8 +261,7 @@
         slot, peer = (1, y_peer) if k % 2 == 0 else (2, x_peer)
         return remote(dmix.at[slot, owner_at(k)], dmix.at[3, owner_at(k)], d_send.at[k], d_recv.at[k], {"dp": peer})
 
-    for k in range(1, tp):
-        col_copy(k).start()
+    col_copies, col_ins = exchange(lambda place: dmix.at[0, me], dmix.at[0], col_send, col_recv)
     x_copy(0).start()
     y_copy(0).start()
     res_ref[...] = (xhat * gain).astype(jnp.bfloat16)
@@ -228,7 +269,7 @@
         copy.wait_recv()
     for k in range(tp + 1):
         if 0 < k < tp:
-            col_arrival(k).wait_recv()
+            col_ins[k - 1].wait_recv()
             x_copy(k).start()
             y_copy(k).start()
         if k > 0:
@@ -260,11 +301,10 @@
             def _():
                 for c in range(CHUNKS):
                     hop(way, d, c).wait_send()
-    for copy in hid_copies + part_copies + stat_copies:
+    for copy in hid_copies + part_copies + stat_copies + col_copies:
         copy.wait_send()
     for k in range(1, tp):
         lcb_copy(k).wait_send()
-        col_copy(k).wait_send()
     for k in range(tp):
         x_copy(k).wait_send()
         y_copy(k).wait_send()
@@ -278,36 +318,27 @@
     rows = samples * tp
     group = w_down.shape[1] // tp
     hidden = w_up.shape[1]
-    pairs = jnp.einsum(
-        "sef,fk->sek", embeddings, projection, preferred_element_type=jnp.float32
-    ).astype(jnp.bfloat16)
-    inter = jnp.einsum(
-        "sek,sef->skf", pairs, embeddings, preferred_element_type=jnp.float32
-    )
-    center = inter - jnp.mean(inter, axis=(1, 2), keepdims=True)
-    spread = jnp.mean(center * center, axis=(1, 2), keepdims=True)
-    normed = (center / jnp.sqrt(spread + EPS)).astype(jnp.bfloat16)
-    lcb = jnp.einsum(
-        "sef,fj->sje", embeddings, compress, preferred_element_type=jnp.float32
-    ).reshape(samples, tp, group).transpose(1, 0, 2)
     feats = w_up.shape[0] // (2 * CHUNKS)
-    normed = normed.reshape(samples, CHUNKS, 2, feats).transpose(1, 2, 0, 3).reshape(CHUNKS, 2 * samples, feats)
     span = 2 * hidden // dp
     chips = dp // 2
     half = rows // 2
     width = 2 * group
     bf16, f32, dma = jnp.bfloat16, jnp.float32, pltpu.SemaphoreType.DMA
     vmem = pl.BlockSpec(memory_space=pltpu.VMEM)
-    hbm = pl.BlockSpec(memory_space=pl.ANY)
+    hbm = pl.BlockSpec(memory_space=pltpu.HBM)
     return pl.pallas_call(
         functools.partial(fused_kernel, dp, tp, samples, rows, group),
         out_shape=(
             jax.ShapeDtypeStruct((rows, width), bf16),
             jax.ShapeDtypeStruct((span // 2, w_down.shape[1]), f32),
         ),
-        in_specs=[vmem, vmem, hbm, hbm, vmem, vmem],
+        in_specs=[hbm, vmem, vmem, hbm, hbm, vmem, vmem],
         out_specs=(vmem, vmem),
         scratch_shapes=[
+            pltpu.VMEM(embeddings.shape, bf16),
+            pltpu.VMEM((embeddings.shape[2] // 128, samples * projection.shape[1], 128), f32),
+            pltpu.VMEM((pl.cdiv(group, 128), samples * 8, 128), f32),
+            pltpu.VMEM((tp, samples, group), f32),
             pltpu.VMEM(w_up.shape, bf16),
             pltpu.VMEM(w_down.shape, bf16),
             pltpu.VMEM((CHUNKS, tp * 2 * samples, feats), bf16),
@@ -322,6 +353,7 @@
             pltpu.VMEM((chips, tp, half, width), bf16),
             pltpu.VMEM((span // 2, w_down.shape[1]), bf16),
             pltpu.VMEM((span // 2, w_down.shape[1]), bf16),
+            dma((3 if samples % 3 == 0 else 1,)),
             dma((CHUNKS + 1,)),
             dma((2, tp, CHUNKS)), dma((2, tp, CHUNKS)),
             dma((tp,)), dma((tp,)),
@@ -335,20 +367,22 @@
             dma, dma,
         ],
         compiler_params=pltpu.CompilerParams(
-            collective_id=0, has_side_effects=True, vmem_limit_bytes=48 * 1024 * 1024
+            collective_id=0, has_side_effects=True, vmem_limit_bytes=65_800_000
         ),
         name="block",
-    )(normed, lcb, w_up, w_down, output_norm_gain.reshape(1, width), out_grad)
+    )(embeddings, projection.T, compress.T, w_up, w_down, output_norm_gain.reshape(1, width), out_grad)
 
 
 def fits(dp, tp, args):
-    embeddings, w_up, w_down = args[0], args[3], args[4]
+    embeddings, projection, compress, w_up, w_down = args[:5]
     if dp != 8 or tp < 2 or embeddings.shape[0] % (dp * tp):
         return False
     samples = embeddings.shape[0] // (dp * tp)
     rows, group, hidden = samples * tp, w_down.shape[1] // tp, w_up.shape[1] // tp
     return (
-        samples % 8 == 0 and rows % 32 == 0 and rows <= 128 and group % 64 == 0
+        compress.shape[1] == tp and embeddings.shape[1] == w_down.shape[1] // tp and tp <= 8
+        and projection.shape[1] % (2 * CHUNKS) == 0 and projection.shape[1] % 16 == 0 and embeddings.shape[2] % 128 == 0
+        and samples % 8 == 0 and rows % 32 == 0 and rows <= 128 and group % 64 == 0
         and hidden % (128 * dp) == 0 and w_up.shape[0] % (256 * CHUNKS) == 0
     )
 

time: 56 us -> 58.2 us (1.039)
  Pallas kernels: 47.3 us -> 52.8 us
  matrix products: 2.52 us -> 0 us
    pallas_call x1, Pallas kernels: 47.3 us -> 52.8 us  [fused_device(): pl.pallas_call(functools.partial(fused_kernel, dp, tp, samples, rows, gro...]
    dot_general x2 -> x0, matrix products: 2.52 us -> none  [the longest x1 1.38 us: fused_device(): jnp.einsum('sef,fj->sje', embeddings, compress, preferred_element_type=jn...]
    unnamed x10 -> x2, local copies, waits for them, and re-layouts: 3.63 us -> 3.29 us
where the time goes in v2:
time: 58.2 us; the launch traced here: 58 us
  Pallas kernels  52.8 us (91%)
  local copies, waits for them, and re-layouts  4.54 us (8%)
  between operations  0.64 us (1%)
    pallas_call x1, Pallas kernels, fused_device(): pl.pallas_call(functools.partial(fused_kernel, dp, tp, samples, rows, gro...  52.8 us
    unnamed x2, local copies, waits for them, and re-layouts  3.29 us
    reshape x1, local copies, waits for them, and re-layouts, fused_device(): output_norm_gain.reshape(1, width)  1.25 us

profile of v2, /device:TPU:0, one launch (start us, length us, event | category | flops | bytes accessed | tf_op | source)
XLA Modules:
  0.0 58.0 jit_solution(8167429833341643355)
XLA Ops:
  0.6 1.2 %reshape.7.gain_ref = f32[1,384]{1,0:T(1,128)} reshape(f32[384]{0:T(512)} %param.12) | data formatting | bytes 3072 | tf_op jit(solution)/shard_map/reshape | solution.py:373
  1.9 52.8 %block.1 = (bf16[96,384]{1,0:T(8,128)(2,1)}, f32[128,768]{1,0:T(8,128)}) custom-call(bf16[24,192,256]{2,1,0:T(8,128)(2,1)} %emb_hbm.1, bf16[16,256]{1,0:T(8,128)(2,1)} %bitcast.2, bf16[4,256]{1,0:T(4,128)(2,1)} %bitcast.3, bf16[4096,1024]{1,0:T(8,128)(2,1)} %up_hbm.1, bf16[1024,768]{1,0:T(8,128)(2,1)} %down_hbm.1, f32[1,384]{1,0:T(1,128)} %reshape.7.gain_ref, ...), custom_call_target="tpu_custom_call" | custom-call | tf_op jit(solution)/shard_map/block/pallas_call | solution.py:329
  54.7 1.5 %copy.11 = bf16[96,384]{1,0:T(8,128)(2,1)} copy(bf16[96,384]{1,0:T(8,128)(2,1)} %get-tuple-element.4) | data formatting | bytes 147456
  56.2 1.8 %copy.12 = f32[128,768]{1,0:T(8,128)} copy(f32[128,768]{1,0:T(8,128)} %get-tuple-element.5) | data formatting | bytes 786432

commit v3 on v1

--- a/solution.py
+++ b/solution.py
@@ -42,7 +42,14 @@
     for load in loads:
         load.start()
 
-    peers = [{"tp": lax.rem(me + k, tp)} for k in range(1, tp)]
+    order = [me]
+    for k in range(1, tp):
+        place = me * 0
+        for t in range(tp):
+            near = sorted(range(tp), key=lambda other: (abs(other - t), other))
+            place = place + jnp.where(me == t, near[k], 0)
+        order.append(place)
+    peers = [{"tp": place} for place in order[1:]]
     others = [{"dp": x_peer}, {"dp": y_peer}, {"dp": d_peer}, {"dp": c_peer}]
     barrier = pltpu.get_barrier_semaphore()
     for peer in peers + others:
@@ -89,11 +96,11 @@
     lcb_in[me] = lcb_ref[me]
 
     def lcb_copy(k):
-        return remote(lcb_ref.at[lax.rem(me + k, tp)], lcb_in.at[me], lcb_send.at[k], lcb_recv.at[k], peers[k - 1])
+        return remote(lcb_ref.at[order[k]], lcb_in.at[me], lcb_send.at[k], lcb_recv.at[me], peers[k - 1])
 
     def lcb_arrival(k):
-        src = lax.rem(me - k + tp, tp)
-        return remote(lcb_in.at[src], lcb_in.at[src], lcb_send.at[k], lcb_recv.at[k], peers[k - 1])
+        src = order[k]
+        return remote(lcb_in.at[src], lcb_in.at[src], lcb_send.at[k], lcb_recv.at[src], peers[k - 1])
 
     for d in range(1, tp):
         if d == tp - 1:
@@ -141,12 +148,17 @@
     for g in range(tp):
         piece = mlp[:, g * group:(g + 1) * group]
         part[g] = jnp.concatenate([piece[:half], piece[half:]], axis=1).astype(jnp.bfloat16)
-    part_copies = [
-        remote(part.at[lax.rem(me + k, tp)], part_in.at[k], part_send.at[k], part_recv.at[k], peers[k - 1])
-        for k in range(1, tp)
-    ]
-    for copy in part_copies:
-        copy.start()
+    def exchange(source, landing, send, recv):
+        outs = [remote(source(order[k]), landing.at[me], send.at[k], recv.at[me], peers[k - 1]) for k in range(1, tp)]
+        ins = [
+            remote(landing.at[order[k]], landing.at[order[k]], send.at[k], recv.at[order[k]], peers[k - 1])
+            for k in range(1, tp)
+        ]
+        for copy in reversed(outs):
+            copy.start()
+        return outs, ins
+
+    part_copies, part_ins = exchange(lambda place: part.at[place], part_in, part_send, part_recv)
 
     gain = gain_ref[...]
     gg = cot_ref[...].astype(jnp.float32) * gain
@@ -154,8 +166,8 @@
         lcb_arrival(k).wait_recv()
     packed = part[me].astype(jnp.float32)
     for k in range(1, tp):
-        part_copies[k - 1].wait_recv()
-        packed += part_in[k].astype(jnp.float32)
+        part_ins[k - 1].wait_recv()
+        packed += part_in[order[k]].astype(jnp.float32)
     summed = jnp.concatenate([packed[:, :group], packed[:, group:]], axis=0)
     linear = jnp.concatenate([lcb_in[t] for t in range(tp)], axis=0)
     mix = jnp.concatenate([summed, linear], axis=1)
@@ -170,15 +182,11 @@
     if rows < 128:
         table = jnp.concatenate([table, jnp.zeros((128 - rows, 128), jnp.float32)], axis=0)
     stat[...] = table.T[:8]
-    stat_copies = [
-        remote(stat, stat_in.at[k], stat_send.at[k], stat_recv.at[k], peers[k - 1]) for k in range(1, tp)
-    ]
-    for copy in stat_copies:
-        copy.start()
+    stat_copies, stat_ins = exchange(lambda place: stat, stat_in, stat_send, stat_recv)
     tables = [stat[...]]
     for k in range(1, tp):
-        stat_copies[k - 1].wait_recv()
-        tables.append(stat_in[k])
+        stat_ins[k - 1].wait_recv()
+        tables.append(stat_in[order[k]])
     full = float(tp * width)
     mean_all = sum(t[0:1] for t in tables) * (1.0 / tp)
     dev_all = sum(t[1:2] + (t[0:1] - mean_all) * (t[0:1] - mean_all) * float(width) for t in tables)
@@ -194,14 +202,7 @@
     dmix[0, me] = jnp.concatenate([grad[:half], grad[half:]], axis=1).astype(jnp.bfloat16)
 
     def owner_at(k):
-        return lax.rem(me + k, tp)
-
-    def col_copy(k):
-        return remote(dmix.at[0, me], dmix.at[0, me], col_send.at[k], col_recv.at[k], peers[k - 1])
-
-    def col_arrival(k):
-        ref = dmix.at[0, owner_at(k)]
-        return remote(ref, ref, col_send.at[tp - k], col_recv.at[tp - k], peers[k - 1])
+        return order[k]
 
     def x_copy(k):
         return remote(dmix.at[0, owner_at(k)], dmix.at[1, owner_at(k)], x_send.at[k], x_recv.at[k], {"dp": x_peer})
@@ -219,8 +220,7 @@
         slot, peer = (1, y_peer) if k % 2 == 0 else (2, x_peer)
         return remote(dmix.at[slot, owner_at(k)], dmix.at[3, owner_at(k)], d_send.at[k], d_recv.at[k], {"dp": peer})
 
-    for k in range(1, tp):
-        col_copy(k).start()
+    col_copies, col_ins = exchange(lambda place: dmix.at[0, me], dmix.at[0], col_send, col_recv)
     x_copy(0).start()
     y_copy(0).start()
     res_ref[...] = (xhat * gain).astype(jnp.bfloat16)
@@ -228,7 +228,7 @@
         copy.wait_recv()
     for k in range(tp + 1):
         if 0 < k < tp:
-            col_arrival(k).wait_recv()
+            col_ins[k - 1].wait_recv()
             x_copy(k).start()
             y_copy(k).start()
         if k > 0:
@@ -260,11 +260,10 @@
             def _():
                 for c in range(CHUNKS):
                     hop(way, d, c).wait_send()
-    for copy in hid_copies + part_copies + stat_copies:
+    for copy in hid_copies + part_copies + stat_copies + col_copies:
         copy.wait_send()
     for k in range(1, tp):
         lcb_copy(k).wait_send()
-        col_copy(k).wait_send()
     for k in range(tp):
         x_copy(k).wait_send()
         y_copy(k).wait_send()

time: 56 us -> 54.5 us (0.973)
  Pallas kernels: 47.3 us -> 45.9 us
    pallas_call x1, Pallas kernels: 47.3 us -> 45.9 us  [fused_device(): pl.pallas_call(functools.partial(fused_kernel, dp, tp, samples, rows, gro...]
where the time goes in v3:
time: 54.5 us; the launch traced here: 54.3 us
  Pallas kernels  45.9 us (84%)
  local copies, waits for them, and re-layouts  4.69 us (9%)
  matrix products  2.52 us (5%)
  between operations  0.72 us (1%)
  other arithmetic  0.55 us (1%)
    pallas_call x1, Pallas kernels, fused_device(): pl.pallas_call(functools.partial(fused_kernel, dp, tp, samples, rows, gro...  45.9 us
    unnamed x10, local copies, waits for them, and re-layouts  3.63 us
    dot_general x1, matrix products, fused_device(): jnp.einsum('sef,fj->sje', embeddings, compress, preferred_element_type=jn...  1.38 us
    dot_general x1, matrix products, fused_device(): jnp.einsum('sek,sef->skf', pairs, embeddings, preferred_element_type=jnp....  1.14 us

profile of v3, /device:TPU:0, one launch (start us, length us, event | category | flops | bytes accessed | tf_op | source)
XLA Modules:
  0.0 54.3 jit_solution(14867224201012482823)
XLA Ops:
  0.6 0.0 copy-start
  0.6 0.0 copy-start.3
  0.7 0.8 %reshape.27.gain_ref = f32[1,384]{1,0:T(1,128)S(1)} reshape(f32[384]{0:T(512)} %param.12) | data formatting | bytes 3072 | tf_op jit(solution)/shard_map/reshape | solution.py:340
  1.5 0.8 %copy-done = bf16[24,192,256]{2,1,0:T(8,128)(2,1)S(1)} copy-done((bf16[24,192,256]{2,1,0:T(8,128)(2,1)S(1)}, bf16[24,192,256]{2,1,0:T(8,128)(2,1)}, u32[]{:S(2)}) %copy-start) | copy-done | bytes 2359320
  2.3 1.4 %fusion.3 = f32[4,24,192]{2,0,1:T(4,128)S(1)} fusion(bf16[24,192,256]{2,1,0:T(8,128)(2,1)S(1)} %copy-done, bf16[256,4]{0,1:T(4,128)(2,1)} %param.9), kind=kOutput, calls=%fused_computation.5 | convolution fusion | flops 9437184 | bytes 2435072 | tf_op jit(solution)/shard_map/sef,fj->sje/dot_general | solution.py:289
  3.7 0.0 copy-done.3
  3.8 0.0 copy-start.2
  3.8 1.1 %fusion.5 = (f32[24]{0:T(128)S(1)}, f32[24,16,256]{2,1,0:T(8,128)S(1)}) fusion(bf16[24,192,256]{2,1,0:T(8,128)(2,1)S(1)} %copy-done, bf16[256,16]{0,1:T(8,128)(2,1)S(1)} %copy-done.3), kind=kOutput, calls=%fused_computation.9 | convolution fusion | flops 75669480 | bytes 2760800 | tf_op jit(solution)/shard_map/sek,sef->skf/dot_general | solution.py:283
  4.9 0.4 multiply_reduce_fusion
  5.3 0.1 divide_convert_fusion
  5.5 0.1 reshape.25
  5.6 0.1 copy.9
  5.7 0.0 copy-done.2
  5.7 0.0 copy-start.1
  5.7 1.4 %copy-done.1 = bf16[1024,768]{1,0:T(8,128)(2,1)S(1)} copy-done((bf16[1024,768]{1,0:T(8,128)(2,1)S(1)}, bf16[1024,768]{1,0:T(8,128)(2,1)}, u32[]{:S(2)}) %copy-start.1) | copy-done | bytes 1572888
  7.1 45.9 %block.1 = (bf16[96,384]{1,0:T(8,128)(2,1)S(1)}, f32[128,768]{1,0:T(8,128)S(1)}) custom-call(bf16[4,48,512]{2,1,0:T(8,128)(2,1)S(1)} %bitcast.15, f32[4,24,192]{2,1,0:T(8,128)S(1)} %copy.10.lcb_ref, bf16[4096,1024]{1,0:T(8,128)(2,1)} %up_hbm.1, bf16[1024,768]{1,0:T(8,128)(2,1)S(1)} %copy-done.1, f32[1,384]{1,0:T(1,128)S(1)} %reshape.27.gain_ref, ...), custom_call_target="tpu_custom_call" | custom-call | tf_op jit(solution)/shard_map/block/pallas_call | solution.py:301
  53.0 0.6 %copy.13 = bf16[96,384]{1,0:T(8,128)(2,1)} copy(bf16[96,384]{1,0:T(8,128)(2,1)S(1)} %get-tuple-element.6) | data formatting | bytes 147456
  53.6 0.7 %copy.14 = f32[128,768]{1,0:T(8,128)} copy(f32[128,768]{1,0:T(8,128)S(1)} %get-tuple-element.7) | data formatting | bytes 786432
  (3 shorter events, 0.1 us)
Async XLA Ops:
  0.6 1.7 %copy-start = (bf16[24,192,256]{2,1,0:T(8,128)(2,1)S(1)}, bf16[24,192,256]{2,1,0:T(8,128)(2,1)}, u32[]{:S(2)}) copy-start(bf16[24,192,256]{2,1,0:T(8,128)(2,1)} %param.7) | copy-start | bytes 7077892
  0.6 3.1 %copy-start.3 = (bf16[256,16]{0,1:T(8,128)(2,1)S(1)}, bf16[256,16]{0,1:T(8,128)(2,1)}, u32[]{:S(2)}) copy-start(bf16[256,16]{0,1:T(8,128)(2,1)} %param.8) | copy-start | bytes 24580
  3.8 1.9 %copy-start.2 = (bf16[96,384]{1,0:T(8,128)(2,1)S(1)}, bf16[96,384]{1,0:T(8,128)(2,1)}, u32[]{:S(2)}) copy-start(bf16[96,384]{1,0:T(8,128)(2,1)} %cot_ref.1) | copy-start | bytes 221188
  5.7 1.4 %copy-start.1 = (bf16[1024,768]{1,0:T(8,128)(2,1)S(1)}, bf16[1024,768]{1,0:T(8,128)(2,1)}, u32[]{:S(2)}) copy-start(bf16[1024,768]{1,0:T(8,128)(2,1)} %down_hbm.1) | copy-start | bytes 4718596
